TPU v7x, 16 devices: a whole 2x2x2 slice. The times are simulated.
16 devices in a mesh: dp: 2 (over z), cp: 8 (over y, x, core).
Axes of the slice: x: 2, y: 2, z: 2, core: 2. Of those that a mesh axis runs over, the one named last changes fastest.
Arguments:
- images: bfloat16 [64, 576, 1024], P('dp', 'cp'), parts along dimension 0
- ln1_scale: float32 [1024], replicated
- ln1_bias: float32 [1024], replicated
- w_qkv: bfloat16 [1024, 3, 16, 64], replicated
- b_qkv: float32 [3, 16, 64], replicated
- w_out: bfloat16 [16, 64, 1024], replicated
- b_out: float32 [1024], replicated
- ln2_scale: float32 [1024], replicated
- ln2_bias: float32 [1024], replicated
- w_up: bfloat16 [1024, 4096], replicated
- b_up: float32 [4096], replicated
- w_down: bfloat16 [4096, 1024], replicated
- b_down: float32 [1024], replicated
- lnf_scale: float32 [1024], replicated
- lnf_bias: float32 [1024], replicated
- pool_probe: bfloat16 [1, 1024], replicated
- pool_wq: bfloat16 [1024, 16, 64], replicated
- pool_bq: float32 [16, 64], replicated
- pool_wkv: bfloat16 [1024, 2, 16, 64], replicated
- pool_bkv: float32 [2, 16, 64], replicated
- pool_wout: bfloat16 [16, 64, 1024], replicated
- pool_bout: float32 [1024], replicated
- pool_ln_scale: float32 [1024], replicated
- pool_ln_bias: float32 [1024], replicated
- pool_w_up: bfloat16 [1024, 4096], replicated
- pool_b_up: float32 [4096], replicated
- pool_w_down: bfloat16 [4096, 1024], replicated
- pool_b_down: float32 [1024], replicated
Outputs:
- output: float32 [64, 1024], P('dp'), parts along dimension 0
There are 2 independent parts. A program takes and returns all parts, laid end to end along the dimension named above; an argument that names none is the same for every part.
All inputs are finite; a program needn't handle non-finite values.
Results may differ from a plain program's by a relative error of at most 0.00933342.
Values are sent between devices in bfloat16 or wider.
A program may use at most 1 GiB of HBM per device.

v0:
```python
import functools

import jax
import jax.numpy as jnp
from jax import lax
from jax.experimental import pallas as pl
from jax.experimental.pallas import tpu as pltpu
from jax.sharding import PartitionSpec as P

EPSILON = 1e-6
MESH = pl.DeviceIdType.MESH
BF16 = jnp.bfloat16
F32 = jnp.float32
LOG2E = 1.4426950408889634
CONTRACT_LAST = (((1,), (1,)), ((), ()))
CONTRACT_FIRST = (((0,), (0,)), ((), ()))

V_LN1S, V_LN1B, V_BQKV, V_BOUT, V_LN2S, V_LN2B, V_BUP, V_BDOWN = 0, 1, 2, 5, 6, 7, 8, 12
V_LNFS, V_LNFB, V_PBQ, V_PBKV, V_PBOUT, V_PLNS, V_PLNB, V_PBUP, V_PBDOWN = 13, 14, 15, 16, 18, 19, 20, 21, 25
V_ROWS = 26


def layer_norm(values, ln_gain, ln_shift):
    row_mean = jnp.mean(values, axis=-1, keepdims=True)
    centered = values - row_mean
    variance = jnp.mean(centered * centered, axis=-1, keepdims=True)
    return centered * lax.rsqrt(variance + EPSILON) * ln_gain + ln_shift


def gelu(x):
    c0 = 0.7978845608028654
    return (0.5 * x) * (1.0 + jnp.tanh(x * (c0 + (c0 * 0.044715) * (x * x))))


def dot_t(lhs, rhs):
    return lax.dot_general(lhs, rhs, CONTRACT_LAST, preferred_element_type=F32)


def dot(lhs, rhs):
    return jnp.dot(lhs, rhs, preferred_element_type=F32)


def kernel(group, own, run, images, vec, probe, wqkv_hbm, wout_hbm, wup_hbm, wdown_hbm, pwq_hbm, pwkv_hbm, pwout_hbm, pwup_hbm, pwdown_hbm,
           out_ref, xbuf, wqkv, wout, wup, wdown, pwq, pwkv, hbuf, qkv, ctx, rbuf, mbuf, acc, ublk, abuf, emb, gath,
           send_sem, recv_sem, w_sem, gsend_sem, grecv_sem):
    me = lax.axis_index("cp")
    width = 1024
    rows = group * run
    pair = 2 * run
    n_pair = group // 2

    def vrow(k):
        return vec[pl.ds(k, 1), :]

    def peer(step):
        return lax.rem(me + step, group)

    weights = ((wqkv_hbm, wqkv), (pwq_hbm, pwq), (wout_hbm, wout), (wup_hbm, wup), (wdown_hbm, wdown), (pwkv_hbm, pwkv),
               (pwout_hbm, wout), (pwup_hbm, wup), (pwdown_hbm, wdown))

    def load(k):
        return pltpu.make_async_copy(weights[k][0], weights[k][1], w_sem.at[k])

    def piece(img, step):
        dst = peer(step)
        return pltpu.make_async_remote_copy(
            src_ref=images.at[dst * own + img], dst_ref=xbuf.at[img, me],
            send_sem=send_sem.at[img, step], recv_sem=recv_sem.at[img, me],
            device_id={"cp": dst}, device_id_type=MESH)

    def local_piece(img):
        return pltpu.make_async_copy(images.at[me * own + img], xbuf.at[img, me], recv_sem.at[img, me])

    load(0).start()
    load(1).start()
    barrier = pltpu.get_barrier_semaphore()
    for step in range(1, group):
        pl.semaphore_signal(barrier, inc=1, device_id={"cp": peer(step)}, device_id_type=MESH)
    pl.semaphore_wait(barrier, group - 1)

    def send_image(img, carry):
        local_piece(img).start()
        for step in (6, 2, 4, 7, 3, 5, 1):
            piece(img, step).start()
        return carry

    lax.fori_loop(0, own, send_image, 0)
    for k in range(2, 6):
        load(k).start()

    load(1).wait()
    probe_rows = jnp.broadcast_to(probe[...], (16, width))
    u = (dot_t(probe_rows, pwq[...]) + vrow(V_PBQ)).astype(BF16).astype(F32)
    head_of_lane = lax.broadcasted_iota(jnp.int32, (16, width), 1) // 64
    head_of_row = lax.broadcasted_iota(jnp.int32, (16, width), 0)
    own_head = head_of_lane == head_of_row
    ublk[...] = jnp.concatenate([jnp.where(own_head, u, 0.0), jnp.zeros((112, width), F32)], axis=0).astype(BF16)
    abuf[...] = jnp.zeros_like(abuf)

    def x_pair(img, pp):
        return jnp.concatenate([xbuf[img, 2 * pp].astype(F32), xbuf[img, 2 * pp + 1].astype(F32)], axis=0)

    def one_image(img, carry):
        first = img == 0
        last = img == own - 1

        for src in range(group):
            pltpu.make_async_copy(images.at[0], xbuf.at[img, src], recv_sem.at[img, src]).wait()
        for pp in range(n_pair):
            hbuf[pl.ds(pp * pair, pair), :] = layer_norm(x_pair(img, pp), vrow(V_LN1S), vrow(V_LN1B)).astype(BF16)

        @pl.when(first)
        def _():
            load(0).wait()

        def project(c, carry):
            qkv[c] = (dot_t(hbuf[...], wqkv[c]) + vec[pl.ds(V_BQKV + c, 1), :]).astype(BF16)
            return carry

        lax.fori_loop(0, 3, project, 0)

        lane = lax.broadcasted_iota(jnp.int32, (1, 128), 1)
        low = (lane < 64).astype(F32)
        low_b = low.astype(BF16)
        high_b = (1.0 - low).astype(BF16)
        score_mul = LOG2E * 0.125

        def head_pair(hp, carry):
            cols = pl.ds(pl.multiple_of(hp * 128, 128), 128)
            q2, k2, v2 = qkv[0, :, cols], qkv[1, :, cols], qkv[2, :, cols]

            def soft(q_half):
                scores = dot_t(q_half, k2)
                top = jnp.max(scores, axis=-1, keepdims=True)
                weight = jnp.exp2((scores - top) * score_mul)
                return weight.astype(BF16), jnp.sum(weight, axis=-1, keepdims=True)

            w_lo, l_lo = soft(q2 * low_b)
            w_hi, l_hi = soft(q2 * high_b)
            total = dot(w_lo, v2 * low_b) + dot(w_hi, v2 * high_b)
            denom = jnp.where(lane < 64, l_lo, l_hi)
            ctx[:, cols] = (total / denom).astype(BF16)
            return carry

        lax.fori_loop(0, 8, head_pair, 0)

        @pl.when(first)
        def _():
            load(2).wait()

        @pl.when(last & (own > 1))
        def _():
            pass

        acc[...] = dot(ctx[...], wout[...])

        @pl.when(last)
        def _():
            load(6).start()

        for pp in range(n_pair):
            block = pl.ds(pp * pair, pair)
            r = (x_pair(img, pp) + (acc[block, :] + vrow(V_BOUT))).astype(BF16)
            rbuf[block, :] = r
            hbuf[block, :] = layer_norm(r.astype(F32), vrow(V_LN2S), vrow(V_LN2B)).astype(BF16)

        @pl.when(first)
        def _():
            load(3).wait()
            load(4).wait()

        acc[...] = rbuf[...].astype(F32) + vrow(V_BDOWN)

        def hidden_chunk(c, carry):
            up = dot(hbuf[...], wup[:, pl.ds(pl.multiple_of(c * 1024, 1024), 1024)]) + vec[pl.ds(V_BUP + c, 1), :]
            mbuf[...] = gelu(up).astype(BF16)
            acc[...] += dot(mbuf[...], wdown[c])
            return carry

        lax.fori_loop(0, 4, hidden_chunk, 0)

        @pl.when(last)
        def _():
            load(7).start()
            load(8).start()

        for pp in range(n_pair):
            block = pl.ds(pp * pair, pair)
            y = acc[block, :].astype(BF16).astype(F32)
            hbuf[block, :] = layer_norm(y, vrow(V_LNFS), vrow(V_LNFB)).astype(BF16)

        @pl.when(first)
        def _():
            load(5).wait()

        def pool_project(c, carry):
            qkv[c] = (dot_t(hbuf[...], pwkv[c]) + vec[pl.ds(V_PBKV + c, 1), :]).astype(BF16)
            return carry

        lax.fori_loop(0, 2, pool_project, 0)
        scores = dot_t(qkv[0], ublk[...])
        top = jnp.max(scores, axis=0, keepdims=True)
        weight = jnp.exp2((scores - top) * score_mul)
        wsum = jnp.sum(weight, axis=0, keepdims=True)
        value = lax.dot_general(weight.astype(BF16), qkv[1], CONTRACT_FIRST, preferred_element_type=F32)[:16]
        diag = lax.broadcasted_iota(jnp.int32, (16, 128), 0) == lax.broadcasted_iota(jnp.int32, (16, 128), 1)
        wcol = jnp.sum(jnp.where(diag, jnp.broadcast_to(wsum, (16, 128)), 0.0), axis=1, keepdims=True)
        pooled = jnp.sum(jnp.where(own_head, value / wcol, 0.0), axis=0, keepdims=True)
        abuf[pl.ds(img, 1), :] = pooled
        return carry

    lax.fori_loop(0, own, one_image, 0)

    load(6).wait()
    load(7).wait()
    load(8).wait()
    pooled_out = (dot(abuf[...].astype(BF16), wout[...]) + vrow(V_PBOUT)).astype(BF16).astype(F32)
    normed_out = layer_norm(pooled_out, vrow(V_PLNS), vrow(V_PLNB)).astype(BF16)
    total = pooled_out + vrow(V_PBDOWN)
    for c in range(4):
        up = dot(normed_out, wup[:, c * 1024:(c + 1) * 1024]) + vrow(V_PBUP + c)
        total = total + dot(gelu(up).astype(BF16), wdown[c])
    emb[...] = total[:8]

    def drain(img, carry):
        for step in range(1, group):
            piece(img, step).wait_send()
        return carry

    lax.fori_loop(0, own, drain, 0)

    def share(step):
        return pltpu.make_async_remote_copy(
            src_ref=emb, dst_ref=gath.at[me], send_sem=gsend_sem.at[step], recv_sem=grecv_sem.at[me],
            device_id={"cp": peer(step)}, device_id_type=MESH)

    for step in range(1, group):
        share(step).start()
    gath[me] = emb[...]
    for step in range(1, group):
        src = lax.rem(me + step, group)
        pltpu.make_async_copy(emb, gath.at[src], grecv_sem.at[src]).wait()
    for step in range(1, group):
        share(step).wait_send()
    for src in range(group):
        out_ref[src * own:(src + 1) * own, :] = gath[src][:own]


def solution(mesh):
    group = mesh.shape["cp"]

    def device_step(images, ln1_scale, ln1_bias, w_qkv, b_qkv, w_out, b_out, ln2_scale, ln2_bias, w_up, b_up, w_down, b_down, lnf_scale, lnf_bias, pool_probe, pool_wq, pool_bq, pool_wkv, pool_bkv, pool_wout, pool_bout, pool_ln_scale, pool_ln_bias, pool_w_up, pool_b_up, pool_w_down, pool_b_down):
        n_img, run, width = images.shape
        own = n_img // group
        rows = group * run
        vec = jnp.concatenate([v.reshape(-1) for v in (
            ln1_scale, ln1_bias, b_qkv, b_out, ln2_scale, ln2_bias, b_up, b_down, lnf_scale, lnf_bias, pool_bq, pool_bkv,
            pool_bout, pool_ln_scale, pool_ln_bias, pool_b_up, pool_b_down)]).reshape(V_ROWS, width)
        wqkv = w_qkv.transpose(1, 2, 3, 0).reshape(3, width, width)
        pwq = pool_wq.transpose(1, 2, 0).reshape(width, width)
        pwkv = pool_wkv.transpose(1, 2, 3, 0).reshape(2, width, width)
        any_spec = pl.BlockSpec(memory_space=pl.ANY)
        vmem_spec = pl.BlockSpec(memory_space=pltpu.VMEM)
        return pl.pallas_call(
            functools.partial(kernel, group, own, run),
            out_shape=jax.ShapeDtypeStruct((n_img, width), F32),
            in_specs=[any_spec, vmem_spec, vmem_spec] + [any_spec] * 9,
            out_specs=vmem_spec,
            scratch_shapes=[
                pltpu.VMEM((own, group, run, width), BF16),
                pltpu.VMEM((3, width, width), BF16),
                pltpu.VMEM((width, width), BF16),
                pltpu.VMEM((width, 4 * width), BF16),
                pltpu.VMEM((4, width, width), BF16),
                pltpu.VMEM((width, width), BF16),
                pltpu.VMEM((2, width, width), BF16),
                pltpu.VMEM((rows, width), BF16),
                pltpu.VMEM((3, rows, width), BF16),
                pltpu.VMEM((rows, width), BF16),
                pltpu.VMEM((rows, width), BF16),
                pltpu.VMEM((rows, width), BF16),
                pltpu.VMEM((rows, width), F32),
                pltpu.VMEM((128, width), BF16),
                pltpu.VMEM((16, width), F32),
                pltpu.VMEM((8, width), F32),
                pltpu.VMEM((group, 8, width), F32),
                pltpu.SemaphoreType.DMA((own, group)),
                pltpu.SemaphoreType.DMA((own, group)),
                pltpu.SemaphoreType.DMA((9,)),
                pltpu.SemaphoreType.DMA((group,)),
                pltpu.SemaphoreType.DMA((group,)),
            ],
            compiler_params=pltpu.CompilerParams(collective_id=0, has_side_effects=True, vmem_limit_bytes=67043328),
        )(images, vec, pool_probe, wqkv, w_out.reshape(width, width), w_up, w_down.reshape(4, width, width), pwq, pwkv,
          pool_wout.reshape(width, width), pool_w_up, pool_w_down.reshape(4, width, width))

    in_specs = (P("dp", "cp", None),) + (P(),) * 27
    return jax.shard_map(device_step, mesh=mesh, in_specs=in_specs, out_specs=P("dp", None), check_vma=False)
```

profile of v0, /device:TPU:0, one launch (start us, length us, event | category | flops | bytes accessed | tf_op | source)
XLA Modules:
  0.0 180.9 jit_solution(5550159358215805512)
XLA Ops:
  0.0 0.8 reshape.34
  0.8 0.8 reshape.35
  1.6 0.8 reshape.33
  2.4 0.7 constant_dynamic-update-slice_fusion.16
  3.0 0.7 constant_dynamic-update-slice_fusion.15
  3.7 0.7 constant_dynamic-update-slice_fusion.13
  4.4 0.7 constant_dynamic-update-slice_fusion.12
  5.1 0.7 constant_dynamic-update-slice_fusion.11
  5.8 0.7 constant_dynamic-update-slice_fusion.10
  6.5 0.7 constant_dynamic-update-slice_fusion.9
  7.2 0.7 constant_dynamic-update-slice_fusion.8
  7.9 0.7 constant_dynamic-update-slice_fusion.7
  8.6 0.7 constant_dynamic-update-slice_fusion.4
  9.3 0.7 constant_dynamic-update-slice_fusion.3
  10.0 0.7 constant_dynamic-update-slice_fusion.2
  10.7 0.7 constant_dynamic-update-slice_fusion.1
  11.4 0.7 constant_dynamic-update-slice_fusion
  12.1 0.7 reshape.36.vec
  12.7 166.6 %shard_map.262 = f32[32,1024]{1,0:T(8,128)} custom-call(bf16[32,72,1024]{2,1,0:T(8,128)(2,1)} %images.1, f32[26,1024]{1,0:T(8,128)} %reshape.36.vec, bf16[1,1024]{1,0:T(2,128)(2,1)} %probe.1, bf16[3,1024,1024]{2,1,0:T(8,128)(2,1)} %bitcast.15, bf16[1024,1024]{1,0:T(8,128)(2,1)} %bitcast.17, bf16[1024,4096]{1,0:T(8,128)(2,1)} %wup_hbm.1, ...), custom_call_target="tpu_custom_call" | custom-call | tf_op jit(solution)/shard_map/pallas_call | solution.py:264
  179.3 1.6 copy.46
  (3 shorter events, 0.0 us)
where the time goes:
time: 182 us; the launch traced here: 181 us
  Pallas kernels  167 us (92%)
  local copies, waits for them, and re-layouts  14.3 us (8%)
    pallas_call x1, Pallas kernels, device_step(): pl.pallas_call(functools.partial(kernel, group, own, run), out_shape=jax....  167 us
    unnamed x17, local copies, waits for them, and re-layouts  10.6 us

commit v1 on v0

--- a/solution.py
+++ b/solution.py
@@ -15,11 +15,6 @@
 CONTRACT_LAST = (((1,), (1,)), ((), ()))
 CONTRACT_FIRST = (((0,), (0,)), ((), ()))
 
-V_LN1S, V_LN1B, V_BQKV, V_BOUT, V_LN2S, V_LN2B, V_BUP, V_BDOWN = 0, 1, 2, 5, 6, 7, 8, 12
-V_LNFS, V_LNFB, V_PBQ, V_PBKV, V_PBOUT, V_PLNS, V_PLNB, V_PBUP, V_PBDOWN = 13, 14, 15, 16, 18, 19, 20, 21, 25
-V_ROWS = 26
-
-
 def layer_norm(values, ln_gain, ln_shift):
     row_mean = jnp.mean(values, axis=-1, keepdims=True)
     centered = values - row_mean
@@ -40,8 +35,9 @@
     return jnp.dot(lhs, rhs, preferred_element_type=F32)
 
 
-def kernel(group, own, run, images, vec, probe, wqkv_hbm, wout_hbm, wup_hbm, wdown_hbm, pwq_hbm, pwkv_hbm, pwout_hbm, pwup_hbm, pwdown_hbm,
-           out_ref, xbuf, wqkv, wout, wup, wdown, pwq, pwkv, hbuf, qkv, ctx, rbuf, mbuf, acc, ublk, abuf, emb, gath,
+def kernel(group, own, run, images, ln1s, ln1b, bqkv_in, bout, ln2s, ln2b, bup, bdown, lnfs, lnfb, pbq_in, pbkv_in, pbout, plns, plnb, pbup, pbdown,
+           probe, wqkv_hbm, wout_hbm, wup_hbm, wdown_hbm, pwq_hbm, pwkv_hbm, pwout_hbm, pwup_hbm, pwdown_hbm,
+           out_ref, xbuf, wqkv, wout, wup, wdown, pwq, pwkv, hbuf, qkv, ctx, rbuf, mbuf, acc, ublk, bias, abuf, emb, gath,
            send_sem, recv_sem, w_sem, gsend_sem, grecv_sem):
     me = lax.axis_index("cp")
     width = 1024
@@ -49,9 +45,6 @@
     pair = 2 * run
     n_pair = group // 2
 
-    def vrow(k):
-        return vec[pl.ds(k, 1), :]
-
     def peer(step):
         return lax.rem(me + step, group)
 
@@ -84,13 +77,17 @@
             piece(img, step).start()
         return carry
 
-    lax.fori_loop(0, own, send_image, 0)
+    send_image(0, 0)
     for k in range(2, 6):
         load(k).start()
 
+    for row, (ref, at) in enumerate(((bqkv_in, 0), (bqkv_in, 1), (bqkv_in, 2), (pbkv_in, 0), (pbkv_in, 1), (pbq_in, 0))):
+        table = ref[at]
+        bias[row:row + 1, :] = jnp.concatenate([table[h:h + 1, :] for h in range(16)], axis=1)
+
     load(1).wait()
     probe_rows = jnp.broadcast_to(probe[...], (16, width))
-    u = (dot_t(probe_rows, pwq[...]) + vrow(V_PBQ)).astype(BF16).astype(F32)
+    u = (dot_t(probe_rows, pwq[...]) + bias[5:6, :]).astype(BF16).astype(F32)
     head_of_lane = lax.broadcasted_iota(jnp.int32, (16, width), 1) // 64
     head_of_row = lax.broadcasted_iota(jnp.int32, (16, width), 0)
     own_head = head_of_lane == head_of_row
@@ -106,15 +103,20 @@
 
         for src in range(group):
             pltpu.make_async_copy(images.at[0], xbuf.at[img, src], recv_sem.at[img, src]).wait()
+
+        @pl.when(img + 1 < own)
+        def _():
+            send_image(img + 1, 0)
+
         for pp in range(n_pair):
-            hbuf[pl.ds(pp * pair, pair), :] = layer_norm(x_pair(img, pp), vrow(V_LN1S), vrow(V_LN1B)).astype(BF16)
+            hbuf[pl.ds(pp * pair, pair), :] = layer_norm(x_pair(img, pp), ln1s[...], ln1b[...]).astype(BF16)
 
         @pl.when(first)
         def _():
             load(0).wait()
 
         def project(c, carry):
-            qkv[c] = (dot_t(hbuf[...], wqkv[c]) + vec[pl.ds(V_BQKV + c, 1), :]).astype(BF16)
+            qkv[c] = (dot_t(hbuf[...], wqkv[c]) + bias[pl.ds(c, 1), :]).astype(BF16)
             return carry
 
         lax.fori_loop(0, 3, project, 0)
@@ -148,10 +150,6 @@
         def _():
             load(2).wait()
 
-        @pl.when(last & (own > 1))
-        def _():
-            pass
-
         acc[...] = dot(ctx[...], wout[...])
 
         @pl.when(last)
@@ -160,19 +158,20 @@
 
         for pp in range(n_pair):
             block = pl.ds(pp * pair, pair)
-            r = (x_pair(img, pp) + (acc[block, :] + vrow(V_BOUT))).astype(BF16)
+            r = (x_pair(img, pp) + (acc[block, :] + bout[...])).astype(BF16)
             rbuf[block, :] = r
-            hbuf[block, :] = layer_norm(r.astype(F32), vrow(V_LN2S), vrow(V_LN2B)).astype(BF16)
+            hbuf[block, :] = layer_norm(r.astype(F32), ln2s[...], ln2b[...]).astype(BF16)
 
         @pl.when(first)
         def _():
             load(3).wait()
             load(4).wait()
 
-        acc[...] = rbuf[...].astype(F32) + vrow(V_BDOWN)
+        acc[...] = rbuf[...].astype(F32) + bdown[...]
 
         def hidden_chunk(c, carry):
-            up = dot(hbuf[...], wup[:, pl.ds(pl.multiple_of(c * 1024, 1024), 1024)]) + vec[pl.ds(V_BUP + c, 1), :]
+            cols = pl.ds(pl.multiple_of(c * 1024, 1024), 1024)
+            up = dot(hbuf[...], wup[:, cols]) + bup[:, cols]
             mbuf[...] = gelu(up).astype(BF16)
             acc[...] += dot(mbuf[...], wdown[c])
             return carry
@@ -187,14 +186,14 @@
         for pp in range(n_pair):
             block = pl.ds(pp * pair, pair)
             y = acc[block, :].astype(BF16).astype(F32)
-            hbuf[block, :] = layer_norm(y, vrow(V_LNFS), vrow(V_LNFB)).astype(BF16)
+            hbuf[block, :] = layer_norm(y, lnfs[...], lnfb[...]).astype(BF16)
 
         @pl.when(first)
         def _():
             load(5).wait()
 
         def pool_project(c, carry):
-            qkv[c] = (dot_t(hbuf[...], pwkv[c]) + vec[pl.ds(V_PBKV + c, 1), :]).astype(BF16)
+            qkv[c] = (dot_t(hbuf[...], pwkv[c]) + bias[pl.ds(3 + c, 1), :]).astype(BF16)
             return carry
 
         lax.fori_loop(0, 2, pool_project, 0)
@@ -214,11 +213,11 @@
     load(6).wait()
     load(7).wait()
     load(8).wait()
-    pooled_out = (dot(abuf[...].astype(BF16), wout[...]) + vrow(V_PBOUT)).astype(BF16).astype(F32)
-    normed_out = layer_norm(pooled_out, vrow(V_PLNS), vrow(V_PLNB)).astype(BF16)
-    total = pooled_out + vrow(V_PBDOWN)
+    pooled_out = (dot(abuf[...].astype(BF16), wout[...]) + pbout[...]).astype(BF16).astype(F32)
+    normed_out = layer_norm(pooled_out, plns[...], plnb[...]).astype(BF16)
+    total = pooled_out + pbdown[...]
     for c in range(4):
-        up = dot(normed_out, wup[:, c * 1024:(c + 1) * 1024]) + vrow(V_PBUP + c)
+        up = dot(normed_out, wup[:, c * 1024:(c + 1) * 1024]) + pbup[:, c * 1024:(c + 1) * 1024]
         total = total + dot(gelu(up).astype(BF16), wdown[c])
     emb[...] = total[:8]
 
@@ -253,9 +252,7 @@
         n_img, run, width = images.shape
         own = n_img // group
         rows = group * run
-        vec = jnp.concatenate([v.reshape(-1) for v in (
-            ln1_scale, ln1_bias, b_qkv, b_out, ln2_scale, ln2_bias, b_up, b_down, lnf_scale, lnf_bias, pool_bq, pool_bkv,
-            pool_bout, pool_ln_scale, pool_ln_bias, pool_b_up, pool_b_down)]).reshape(V_ROWS, width)
+        row = lambda v: v.reshape(1, -1)
         wqkv = w_qkv.transpose(1, 2, 3, 0).reshape(3, width, width)
         pwq = pool_wq.transpose(1, 2, 0).reshape(width, width)
         pwkv = pool_wkv.transpose(1, 2, 3, 0).reshape(2, width, width)
@@ -264,7 +261,7 @@
         return pl.pallas_call(
             functools.partial(kernel, group, own, run),
             out_shape=jax.ShapeDtypeStruct((n_img, width), F32),
-            in_specs=[any_spec, vmem_spec, vmem_spec] + [any_spec] * 9,
+            in_specs=[any_spec] + [vmem_spec] * 18 + [any_spec] * 9,
             out_specs=vmem_spec,
             scratch_shapes=[
                 pltpu.VMEM((own, group, run, width), BF16),
@@ -281,6 +278,7 @@
                 pltpu.VMEM((rows, width), BF16),
                 pltpu.VMEM((rows, width), F32),
                 pltpu.VMEM((128, width), BF16),
+                pltpu.VMEM((8, width), F32),
                 pltpu.VMEM((16, width), F32),
                 pltpu.VMEM((8, width), F32),
                 pltpu.VMEM((group, 8, width), F32),
@@ -291,7 +289,9 @@
                 pltpu.SemaphoreType.DMA((group,)),
             ],
             compiler_params=pltpu.CompilerParams(collective_id=0, has_side_effects=True, vmem_limit_bytes=67043328),
-        )(images, vec, pool_probe, wqkv, w_out.reshape(width, width), w_up, w_down.reshape(4, width, width), pwq, pwkv,
+        )(images, row(ln1_scale), row(ln1_bias), b_qkv, row(b_out), row(ln2_scale), row(ln2_bias), row(b_up), row(b_down),
+          row(lnf_scale), row(lnf_bias), pool_bq[None], pool_bkv, row(pool_bout), row(pool_ln_scale), row(pool_ln_bias),
+          row(pool_b_up), row(pool_b_down), pool_probe, wqkv, w_out.reshape(width, width), w_up, w_down.reshape(4, width, width), pwq, pwkv,
           pool_wout.reshape(width, width), pool_w_up, pool_w_down.reshape(4, width, width))
 
     in_specs = (P("dp", "cp", None),) + (P(),) * 27

time: 182 us -> 168 us (0.923)
  local copies, waits for them, and re-layouts: 14.3 us -> 1.57 us
    unnamed x17 -> x1, local copies, waits for them, and re-layouts: 10.6 us -> 1.57 us
    reshape x4 -> x0, local copies, waits for them, and re-layouts: 3.04 us -> none  [the longest x3 2.36 us: device_step(): v.reshape(-1)]
where the time goes in v1:
time: 168 us
  Pallas kernels  166 us (99%)
    pallas_call x1, Pallas kernels, device_step(): pl.pallas_call(functools.partial(kernel, group, own, run), out_shape=jax....  166 us

profile of v1, /device:TPU:0, one launch (start us, length us, event | category | flops | bytes accessed | tf_op | source)
XLA Modules:
  0.0 167.7 jit_solution(16676230306775216488)
XLA Ops:
  0.0 166.1 %shard_map.262 = f32[32,1024]{1,0:T(8,128)} custom-call(bf16[32,72,1024]{2,1,0:T(8,128)(2,1)} %images.1, f32[1,1024]{1,0:T(1,128)} %bitcast.38, f32[1,1024]{1,0:T(1,128)} %bitcast.39, f32[3,16,64]{2,1,0:T(8,128)} %bqkv_in.1, f32[1,1024]{1,0:T(1,128)} %bitcast.40, f32[1,1024]{1,0:T(1,128)} %bitcast.41, f32[1,1024]{1,0:T(1,128)} %bitcast.42, ...), custom_call_target="tpu_custom_call" | custom-call | tf_op jit(solution)/shard_map/pallas_call | solution.py:261
  166.1 1.6 copy.30

commit v2 on v1

v2 whole, which is shorter than its diff:
```python
import functools

import jax
import jax.numpy as jnp
from jax import lax
from jax.experimental import pallas as pl
from jax.experimental.pallas import tpu as pltpu
from jax.sharding import PartitionSpec as P

EPSILON = 1e-6
MESH = pl.DeviceIdType.MESH
BF16 = jnp.bfloat16
F32 = jnp.float32
LOG2E = 1.4426950408889634
CONTRACT_LAST = (((1,), (1,)), ((), ()))
CONTRACT_FIRST = (((0,), (0,)), ((), ()))

def layer_norm(values, ln_gain, ln_shift):
    row_mean = jnp.mean(values, axis=-1, keepdims=True)
    centered = values - row_mean
    variance = jnp.mean(centered * centered, axis=-1, keepdims=True)
    return centered * lax.rsqrt(variance + EPSILON) * ln_gain + ln_shift


def gelu(x):
    c0 = 0.7978845608028654
    return (0.5 * x) * (1.0 + jnp.tanh(x * (c0 + (c0 * 0.044715) * (x * x))))


def dot_t(lhs, rhs):
    return lax.dot_general(lhs, rhs, CONTRACT_LAST, preferred_element_type=F32)


def dot(lhs, rhs):
    return jnp.dot(lhs, rhs, preferred_element_type=F32)


def blocks(ref, count, first=0, rows=slice(None)):
    return jnp.concatenate([ref[first + c, rows, :] for c in range(count)], axis=1)


def put(ref, value, count, first=0, rows=slice(None)):
    for c in range(count):
        ref[first + c, rows, :] = value[:, c * 128:(c + 1) * 128].astype(BF16)


def kernel(group, own, run, images, ln1s, ln1b, bqkv_in, bout, ln2s, ln2b, bup, bdown, lnfs, lnfb, pbq_in, pbkv_in, pbout, plns, plnb, pbup, pbdown,
           probe, wqkv_hbm, wout_hbm, wup_hbm, wdown_hbm, pwq_hbm, pwkv_hbm, pwout_hbm, pwup_hbm, pwdown_hbm,
           out_ref, xbuf, wqkv, wout, wup, wdown, pwkv, hbuf, qkv, ctx, mbuf, acc, ublk, bias, abuf, emb, gath,
           send_sem, recv_sem, w_sem, gsend_sem, grecv_sem):
    me = lax.axis_index("cp")
    width = 1024
    rows = group * run

    def peer(step):
        return lax.rem(me + step, group)

    weights = ((wqkv_hbm, wqkv), (pwq_hbm, pwkv.at[:, :width]), (wout_hbm, wout), (wup_hbm, wup), (wdown_hbm, wdown), (pwkv_hbm, pwkv),
               (pwout_hbm, wout), (pwup_hbm, wup), (pwdown_hbm, wdown))

    def start(k):
        src, dst = weights[k]

        def one(c, carry):
            cols = pl.ds(pl.multiple_of(c * 128, 128), 128)
            pltpu.make_async_copy(src.at[:, cols], dst.at[c], w_sem.at[k]).start()
            return carry

        lax.fori_loop(0, src.shape[1] // 128, one, 0)

    def arrived(k):
        dst = weights[k][1]
        pltpu.make_async_copy(dst, dst, w_sem.at[k]).wait()

    def piece(img, step):
        dst = peer(step)
        return pltpu.make_async_remote_copy(
            src_ref=images.at[dst * own + img], dst_ref=xbuf.at[img, me],
            send_sem=send_sem.at[img, step], recv_sem=recv_sem.at[img, me],
            device_id={"cp": dst}, device_id_type=MESH)

    def local_piece(img):
        return pltpu.make_async_copy(images.at[me * own + img], xbuf.at[img, me], recv_sem.at[img, me])

    start(0)
    start(1)
    barrier = pltpu.get_barrier_semaphore()
    for step in range(1, group):
        pl.semaphore_signal(barrier, inc=1, device_id={"cp": peer(step)}, device_id_type=MESH)
    pl.semaphore_wait(barrier, group - 1)

    def send_image(img, carry):
        local_piece(img).start()
        for step in (6, 2, 4, 7, 3, 5, 1):
            piece(img, step).start()
        return carry

    send_image(0, 0)
    for k in range(2, 5):
        start(k)

    for row, (ref, at) in enumerate(((bqkv_in, 0), (bqkv_in, 1), (bqkv_in, 2), (pbkv_in, 0), (pbkv_in, 1), (pbq_in, 0))):
        table = ref[at]
        bias[row:row + 1, :] = jnp.concatenate([table[h:h + 1, :] for h in range(16)], axis=1)

    arrived(1)
    probe_rows = jnp.broadcast_to(probe[...], (16, width))
    u = (dot_t(probe_rows, blocks(pwkv, 8, rows=slice(0, width))) + bias[5:6, :]).astype(BF16).astype(F32)
    head_of_lane = lax.broadcasted_iota(jnp.int32, (16, width), 1) // 64
    head_of_row = lax.broadcasted_iota(jnp.int32, (16, width), 0)
    own_head = head_of_lane == head_of_row
    put(ublk, jnp.concatenate([jnp.where(own_head, u, 0.0), jnp.zeros((112, width), F32)], axis=0), 8)
    start(5)
    abuf[...] = jnp.zeros_like(abuf)

    chunk = 16

    def x_rows(img, at):
        src, off = at // run, at % run
        if off + chunk <= run:
            return xbuf[img, src, off:off + chunk].astype(F32)
        return jnp.concatenate([xbuf[img, src, off:].astype(F32), xbuf[img, src + 1, :off + chunk - run].astype(F32)], axis=0)

    def one_image(img, carry):
        first = img == 0
        last = img == own - 1

        for src in range(group):
            pltpu.make_async_copy(images.at[0], xbuf.at[img, src], recv_sem.at[img, src]).wait()

        @pl.when(img + 1 < own)
        def _():
            send_image(img + 1, 0)

        for at in range(0, rows, chunk):
            put(hbuf, layer_norm(x_rows(img, at), ln1s[...], ln1b[...]), 8, rows=slice(at, at + chunk))

        @pl.when(first)
        def _():
            arrived(0)

        def project(c, carry):
            weight = blocks(wqkv, 8, rows=pl.ds(pl.multiple_of(c * width, width), width))
            put(qkv, dot_t(blocks(hbuf, 8), weight) + bias[pl.ds(c, 1), :], 8, first=c * 8)
            return carry

        lax.fori_loop(0, 3, project, 0)

        lane = lax.broadcasted_iota(jnp.int32, (1, 128), 1)
        low = (lane < 64).astype(F32)
        low_b = low.astype(BF16)
        high_b = (1.0 - low).astype(BF16)
        score_mul = LOG2E * 0.125

        def head_pair(hp, carry):
            q2, k2, v2 = qkv[hp], qkv[8 + hp], qkv[16 + hp]

            def soft(q_half):
                scores = dot_t(q_half, k2)
                top = jnp.max(scores, axis=-1, keepdims=True)
                weight = jnp.exp2((scores - top) * score_mul)
                return weight.astype(BF16), jnp.sum(weight, axis=-1, keepdims=True)

            w_lo, l_lo = soft(q2 * low_b)
            w_hi, l_hi = soft(q2 * high_b)
            total = dot(w_lo, v2 * low_b) + dot(w_hi, v2 * high_b)
            denom = jnp.where(lane < 64, l_lo, l_hi)
            ctx[hp] = (total / denom).astype(BF16)
            return carry

        lax.fori_loop(0, 8, head_pair, 0)

        @pl.when(first)
        def _():
            arrived(2)

        acc[...] = dot(blocks(ctx, 8), blocks(wout, 8))

        @pl.when(last)
        def _():
            start(6)

        for at in range(0, rows, chunk):
            block = slice(at, at + chunk)
            r = (x_rows(img, at) + (acc[block, :] + bout[...])).astype(BF16).astype(F32)
            acc[block, :] = r + bdown[...]
            put(hbuf, layer_norm(r, ln2s[...], ln2b[...]), 8, rows=block)

        @pl.when(first)
        def _():
            arrived(3)
            arrived(4)

        def hidden_chunk(c, carry):
            cols = pl.ds(pl.multiple_of(c * width, width), width)
            put(mbuf, gelu(dot(blocks(hbuf, 8), blocks(wup, 8, first=c * 8)) + bup[:, cols]), 8)
            acc[...] += dot(blocks(mbuf, 8), blocks(wdown, 8, rows=cols))
            return carry

        lax.fori_loop(0, 4, hidden_chunk, 0)

        @pl.when(last)
        def _():
            start(7)
            start(8)

        for at in range(0, rows, chunk):
            block = slice(at, at + chunk)
            y = acc[block, :].astype(BF16).astype(F32)
            put(hbuf, layer_norm(y, lnfs[...], lnfb[...]), 8, rows=block)

        @pl.when(first)
        def _():
            arrived(5)

        for c in range(2):
            weight = blocks(pwkv, 8, rows=slice(c * width, (c + 1) * width))
            put(qkv, dot_t(blocks(hbuf, 8), weight) + bias[3 + c:4 + c, :], 8, first=c * 8)
        scores = dot_t(blocks(qkv, 8), blocks(ublk, 8))
        top = jnp.max(scores, axis=0, keepdims=True)
        weight = jnp.exp2((scores - top) * score_mul)
        wsum = jnp.sum(weight, axis=0, keepdims=True)
        value = lax.dot_general(weight.astype(BF16), blocks(qkv, 8, first=8), CONTRACT_FIRST, preferred_element_type=F32)[:16]
        diag = lax.broadcasted_iota(jnp.int32, (16, 128), 0) == lax.broadcasted_iota(jnp.int32, (16, 128), 1)
        wcol = jnp.sum(jnp.where(diag, jnp.broadcast_to(wsum, (16, 128)), 0.0), axis=1, keepdims=True)
        pooled = jnp.sum(jnp.where(own_head, value / wcol, 0.0), axis=0, keepdims=True)
        abuf[pl.ds(img, 1), :] = pooled
        return carry

    lax.fori_loop(0, own, one_image, 0)

    arrived(6)
    arrived(7)
    arrived(8)
    pooled_out = (dot(abuf[...].astype(BF16), blocks(wout, 8)) + pbout[...]).astype(BF16).astype(F32)
    normed_out = layer_norm(pooled_out, plns[...], plnb[...]).astype(BF16)
    total = pooled_out + pbdown[...]
    for c in range(4):
        up = dot(normed_out, blocks(wup, 8, first=c * 8)) + pbup[:, c * 1024:(c + 1) * 1024]
        total = total + dot(gelu(up).astype(BF16), blocks(wdown, 8, rows=slice(c * 1024, (c + 1) * 1024)))
    emb[...] = total[:8]

    def drain(img, carry):
        for step in range(1, group):
            piece(img, step).wait_send()
        return carry

    lax.fori_loop(0, own, drain, 0)

    def share(step):
        return pltpu.make_async_remote_copy(
            src_ref=emb, dst_ref=gath.at[me], send_sem=gsend_sem.at[step], recv_sem=grecv_sem.at[me],
            device_id={"cp": peer(step)}, device_id_type=MESH)

    for step in range(1, group):
        share(step).start()
    gath[me] = emb[...]
    for step in range(1, group):
        src = lax.rem(me + step, group)
        pltpu.make_async_copy(emb, gath.at[src], grecv_sem.at[src]).wait()
    for step in range(1, group):
        share(step).wait_send()
    for src in range(group):
        out_ref[src * own:(src + 1) * own, :] = gath[src][:own]


def solution(mesh):
    group = mesh.shape["cp"]

    def device_step(images, ln1_scale, ln1_bias, w_qkv, b_qkv, w_out, b_out, ln2_scale, ln2_bias, w_up, b_up, w_down, b_down, lnf_scale, lnf_bias, pool_probe, pool_wq, pool_bq, pool_wkv, pool_bkv, pool_wout, pool_bout, pool_ln_scale, pool_ln_bias, pool_w_up, pool_b_up, pool_w_down, pool_b_down):
        n_img, run, width = images.shape
        own = n_img // group
        rows = group * run
        row = lambda v: v.reshape(1, -1)
        wqkv = w_qkv.transpose(1, 2, 3, 0).reshape(3 * width, width)
        pwq = pool_wq.transpose(1, 2, 0).reshape(width, width)
        pwkv = pool_wkv.transpose(1, 2, 3, 0).reshape(2 * width, width)
        any_spec = pl.BlockSpec(memory_space=pl.ANY)
        vmem_spec = pl.BlockSpec(memory_space=pltpu.VMEM)
        return pl.pallas_call(
            functools.partial(kernel, group, own, run),
            out_shape=jax.ShapeDtypeStruct((n_img, width), F32),
            in_specs=[any_spec] + [vmem_spec] * 18 + [any_spec] * 9,
            out_specs=vmem_spec,
            scratch_shapes=[
                pltpu.VMEM((own, group, run, width), BF16),
                pltpu.VMEM((8, 3 * width, 128), BF16),
                pltpu.VMEM((8, width, 128), BF16),
                pltpu.VMEM((32, width, 128), BF16),
                pltpu.VMEM((8, 4 * width, 128), BF16),
                pltpu.VMEM((8, 2 * width, 128), BF16),
                pltpu.VMEM((8, rows, 128), BF16),
                pltpu.VMEM((24, rows, 128), BF16),
                pltpu.VMEM((8, rows, 128), BF16),
                pltpu.VMEM((8, rows, 128), BF16),
                pltpu.VMEM((rows, width), F32),
                pltpu.VMEM((8, 128, 128), BF16),
                pltpu.VMEM((8, width), F32),
                pltpu.VMEM((16, width), F32),
                pltpu.VMEM((8, width), F32),
                pltpu.VMEM((group, 8, width), F32),
                pltpu.SemaphoreType.DMA((own, group)),
                pltpu.SemaphoreType.DMA((own, group)),
                pltpu.SemaphoreType.DMA((9,)),
                pltpu.SemaphoreType.DMA((group,)),
                pltpu.SemaphoreType.DMA((group,)),
            ],
            compiler_params=pltpu.CompilerParams(collective_id=0, has_side_effects=True, vmem_limit_bytes=67043328),
        )(images, row(ln1_scale), row(ln1_bias), b_qkv, row(b_out), row(ln2_scale), row(ln2_bias), row(b_up), row(b_down),
          row(lnf_scale), row(lnf_bias), pool_bq[None], pool_bkv, row(pool_bout), row(pool_ln_scale), row(pool_ln_bias),
          row(pool_b_up), row(pool_b_down), pool_probe, wqkv, w_out.reshape(width, width), w_up, w_down, pwq, pwkv,
          pool_wout.reshape(width, width), pool_w_up, pool_w_down)

    in_specs = (P("dp", "cp", None),) + (P(),) * 27
    return jax.shard_map(device_step, mesh=mesh, in_specs=in_specs, out_specs=P("dp", None), check_vma=False)
```

time: 168 us -> 169 us (level)
  Pallas kernels: 166 us -> 168 us
where the time goes in v2:
time: 169 us
  Pallas kernels  168 us (99%)
    pallas_call x1, Pallas kernels, device_step(): pl.pallas_call(functools.partial(kernel, group, own, run), out_shape=jax....  168 us

profile of v2, /device:TPU:0, one launch (start us, length us, event | category | flops | bytes accessed | tf_op | source)
XLA Modules:
  0.0 169.3 jit_solution(14910494393133576942)
XLA Ops:
  0.0 167.7 %shard_map.262 = f32[32,1024]{1,0:T(8,128)} custom-call(bf16[32,72,1024]{2,1,0:T(8,128)(2,1)} %images.1, f32[1,1024]{1,0:T(1,128)} %bitcast.34, f32[1,1024]{1,0:T(1,128)} %bitcast.35, f32[3,16,64]{2,1,0:T(8,128)} %bqkv_in.1, f32[1,1024]{1,0:T(1,128)} %bitcast.36, f32[1,1024]{1,0:T(1,128)} %bitcast.37, f32[1,1024]{1,0:T(1,128)} %bitcast.38, ...), custom_call_target="tpu_custom_call" | custom-call | tf_op jit(solution)/shard_map/pallas_call | solution.py:280
  167.7 1.6 copy.30

commit v3 on v2

--- a/solution.py
+++ b/solution.py
@@ -62,11 +62,11 @@
         src, dst = weights[k]
 
         def one(c, carry):
-            cols = pl.ds(pl.multiple_of(c * 128, 128), 128)
+            cols = pl.ds(pl.multiple_of(c * 512, 512), 512)
             pltpu.make_async_copy(src.at[:, cols], dst.at[c], w_sem.at[k]).start()
             return carry
 
-        lax.fori_loop(0, src.shape[1] // 128, one, 0)
+        lax.fori_loop(0, src.shape[1] // 512, one, 0)
 
     def arrived(k):
         dst = weights[k][1]
@@ -105,7 +105,7 @@
 
     arrived(1)
     probe_rows = jnp.broadcast_to(probe[...], (16, width))
-    u = (dot_t(probe_rows, blocks(pwkv, 8, rows=slice(0, width))) + bias[5:6, :]).astype(BF16).astype(F32)
+    u = (dot_t(probe_rows, blocks(pwkv, 2, rows=slice(0, width))) + bias[5:6, :]).astype(BF16).astype(F32)
     head_of_lane = lax.broadcasted_iota(jnp.int32, (16, width), 1) // 64
     head_of_row = lax.broadcasted_iota(jnp.int32, (16, width), 0)
     own_head = head_of_lane == head_of_row
@@ -139,12 +139,9 @@
         def _():
             arrived(0)
 
-        def project(c, carry):
-            weight = blocks(wqkv, 8, rows=pl.ds(pl.multiple_of(c * width, width), width))
-            put(qkv, dot_t(blocks(hbuf, 8), weight) + bias[pl.ds(c, 1), :], 8, first=c * 8)
-            return carry
-
-        lax.fori_loop(0, 3, project, 0)
+        for c in range(3):
+            weight = blocks(wqkv, 2, rows=slice(c * width, (c + 1) * width))
+            put(qkv, dot_t(blocks(hbuf, 8), weight) + bias[c:c + 1, :], 8, first=c * 8)
 
         lane = lax.broadcasted_iota(jnp.int32, (1, 128), 1)
         low = (lane < 64).astype(F32)
@@ -152,7 +149,7 @@
         high_b = (1.0 - low).astype(BF16)
         score_mul = LOG2E * 0.125
 
-        def head_pair(hp, carry):
+        def one_pair(hp):
             q2, k2, v2 = qkv[hp], qkv[8 + hp], qkv[16 + hp]
 
             def soft(q_half):
@@ -166,43 +163,56 @@
             total = dot(w_lo, v2 * low_b) + dot(w_hi, v2 * high_b)
             denom = jnp.where(lane < 64, l_lo, l_hi)
             ctx[hp] = (total / denom).astype(BF16)
+
+        def head_pair(step, carry):
+            one_pair(2 * step)
+            one_pair(2 * step + 1)
             return carry
 
-        lax.fori_loop(0, 8, head_pair, 0)
+        lax.fori_loop(0, 4, head_pair, 0)
 
         @pl.when(first)
         def _():
             arrived(2)
 
-        acc[...] = dot(blocks(ctx, 8), blocks(wout, 8))
-
-        @pl.when(last)
-        def _():
-            start(6)
-
+        for at in range(0, rows, rows // 2):
+            half = slice(at, at + rows // 2)
+            acc[half, :] = dot(blocks(ctx, 8, rows=half), blocks(wout, 2))
         for at in range(0, rows, chunk):
             block = slice(at, at + chunk)
             r = (x_rows(img, at) + (acc[block, :] + bout[...])).astype(BF16).astype(F32)
             acc[block, :] = r + bdown[...]
             put(hbuf, layer_norm(r, ln2s[...], ln2b[...]), 8, rows=block)
 
+        @pl.when(last)
+        def _():
+            start(6)
+
         @pl.when(first)
         def _():
             arrived(3)
             arrived(4)
 
-        def hidden_chunk(c, carry):
-            cols = pl.ds(pl.multiple_of(c * width, width), width)
-            put(mbuf, gelu(dot(blocks(hbuf, 8), blocks(wup, 8, first=c * 8)) + bup[:, cols]), 8)
-            acc[...] += dot(blocks(mbuf, 8), blocks(wdown, 8, rows=cols))
+        def hidden_chunk(step, carry):
+            spans = [pl.ds(pl.multiple_of((2 * step + i) * width, width), width) for i in range(2)]
+            for i in range(2):
+                up = dot(blocks(hbuf, 8), blocks(wup, 2, first=(2 * step + i) * 2)) + bup[:, spans[i]]
+                put(mbuf, gelu(up), 8, first=8 * i)
+            acc[...] += dot(blocks(mbuf, 8), blocks(wdown, 2, rows=spans[0])) + dot(blocks(mbuf, 8, first=8), blocks(wdown, 2, rows=spans[1]))
+
+            @pl.when(last)
+            def _():
+                for i in range(4):
+                    part = step * 4 + i
+                    up_cols = pl.ds(pl.multiple_of(part * 512, 512), 512)
+                    pltpu.make_async_copy(pwup_hbm.at[:, up_cols], wup.at[part], w_sem.at[7]).start()
+                for i in range(2):
+                    down_rows = pl.ds(pl.multiple_of(step * 2 * width, width), 2 * width)
+                    pltpu.make_async_copy(pwdown_hbm.at[down_rows, i * 512:(i + 1) * 512], wdown.at[i, down_rows], w_sem.at[8]).start()
+
             return carry
 
-        lax.fori_loop(0, 4, hidden_chunk, 0)
-
-        @pl.when(last)
-        def _():
-            start(7)
-            start(8)
+        lax.fori_loop(0, 2, hidden_chunk, 0)
 
         for at in range(0, rows, chunk):
             block = slice(at, at + chunk)
@@ -214,7 +224,7 @@
             arrived(5)
 
         for c in range(2):
-            weight = blocks(pwkv, 8, rows=slice(c * width, (c + 1) * width))
+            weight = blocks(pwkv, 2, rows=slice(c * width, (c + 1) * width))
             put(qkv, dot_t(blocks(hbuf, 8), weight) + bias[3 + c:4 + c, :], 8, first=c * 8)
         scores = dot_t(blocks(qkv, 8), blocks(ublk, 8))
         top = jnp.max(scores, axis=0, keepdims=True)
@@ -232,12 +242,12 @@
     arrived(6)
     arrived(7)
     arrived(8)
-    pooled_out = (dot(abuf[...].astype(BF16), blocks(wout, 8)) + pbout[...]).astype(BF16).astype(F32)
+    pooled_out = (dot(abuf[...].astype(BF16), blocks(wout, 2)) + pbout[...]).astype(BF16).astype(F32)
     normed_out = layer_norm(pooled_out, plns[...], plnb[...]).astype(BF16)
     total = pooled_out + pbdown[...]
     for c in range(4):
-        up = dot(normed_out, blocks(wup, 8, first=c * 8)) + pbup[:, c * 1024:(c + 1) * 1024]
-        total = total + dot(gelu(up).astype(BF16), blocks(wdown, 8, rows=slice(c * 1024, (c + 1) * 1024)))
+        up = dot(normed_out, blocks(wup, 2, first=c * 2)) + pbup[:, c * 1024:(c + 1) * 1024]
+        total = total + dot(gelu(up).astype(BF16), blocks(wdown, 2, rows=slice(c * 1024, (c + 1) * 1024)))
     emb[...] = total[:8]
 
     def drain(img, carry):
@@ -284,15 +294,15 @@
             out_specs=vmem_spec,
             scratch_shapes=[
                 pltpu.VMEM((own, group, run, width), BF16),
-                pltpu.VMEM((8, 3 * width, 128), BF16),
-                pltpu.VMEM((8, width, 128), BF16),
-                pltpu.VMEM((32, width, 128), BF16),
-                pltpu.VMEM((8, 4 * width, 128), BF16),
-                pltpu.VMEM((8, 2 * width, 128), BF16),
+                pltpu.VMEM((2, 3 * width, 512), BF16),
+                pltpu.VMEM((2, width, 512), BF16),
+                pltpu.VMEM((8, width, 512), BF16),
+                pltpu.VMEM((2, 4 * width, 512), BF16),
+                pltpu.VMEM((2, 2 * width, 512), BF16),
                 pltpu.VMEM((8, rows, 128), BF16),
                 pltpu.VMEM((24, rows, 128), BF16),
                 pltpu.VMEM((8, rows, 128), BF16),
-                pltpu.VMEM((8, rows, 128), BF16),
+                pltpu.VMEM((16, rows, 128), BF16),
                 pltpu.VMEM((rows, width), F32),
                 pltpu.VMEM((8, 128, 128), BF16),
                 pltpu.VMEM((8, width), F32),

time: 169 us -> 159 us (0.941)
  Pallas kernels: 168 us -> 158 us
    pallas_call x1, Pallas kernels: 168 us -> 158 us  [device_step(): pl.pallas_call(functools.partial(kernel, group, own, run), out_shape=jax....]
where the time goes in v3:
time: 159 us
  Pallas kernels  158 us (99%)
    pallas_call x1, Pallas kernels, device_step(): pl.pallas_call(functools.partial(kernel, group, own, run), out_shape=jax....  158 us

profile of v3, /device:TPU:0, one launch (start us, length us, event | category | flops | bytes accessed | tf_op | source)
XLA Modules:
  0.0 159.3 jit_solution(16046339243770615440)
XLA Ops:
  0.0 157.7 %shard_map.262 = f32[32,1024]{1,0:T(8,128)} custom-call(bf16[32,72,1024]{2,1,0:T(8,128)(2,1)} %images.1, f32[1,1024]{1,0:T(1,128)} %bitcast.34, f32[1,1024]{1,0:T(1,128)} %bitcast.35, f32[3,16,64]{2,1,0:T(8,128)} %bqkv_in.1, f32[1,1024]{1,0:T(1,128)} %bitcast.36, f32[1,1024]{1,0:T(1,128)} %bitcast.37, f32[1,1024]{1,0:T(1,128)} %bitcast.38, ...), custom_call_target="tpu_custom_call" | custom-call | tf_op jit(solution)/shard_map/pallas_call | solution.py:290
  157.7 1.6 copy.30

commit v4 on v3

--- a/solution.py
+++ b/solution.py
@@ -46,7 +46,7 @@
 
 def kernel(group, own, run, images, ln1s, ln1b, bqkv_in, bout, ln2s, ln2b, bup, bdown, lnfs, lnfb, pbq_in, pbkv_in, pbout, plns, plnb, pbup, pbdown,
            probe, wqkv_hbm, wout_hbm, wup_hbm, wdown_hbm, pwq_hbm, pwkv_hbm, pwout_hbm, pwup_hbm, pwdown_hbm,
-           out_ref, xbuf, wqkv, wout, wup, wdown, pwkv, hbuf, qkv, ctx, mbuf, acc, ublk, bias, abuf, emb, gath,
+           out_ref, xbuf, wqkv, wout, wup, wdown, pwkv, h1, hbuf, qkv, ctx, mbuf, acc, ublk, bias, abuf, emb, gath,
            send_sem, recv_sem, w_sem, gsend_sem, grecv_sem):
     me = lax.axis_index("cp")
     width = 1024
@@ -115,33 +115,44 @@
 
     chunk = 16
 
-    def x_rows(img, at):
-        src, off = at // run, at % run
+    def x_rows(img, at, base=0):
+        src, off = base + at // run, at % run
         if off + chunk <= run:
             return xbuf[img, src, off:off + chunk].astype(F32)
         return jnp.concatenate([xbuf[img, src, off:].astype(F32), xbuf[img, src + 1, :off + chunk - run].astype(F32)], axis=0)
 
+    def landed(img, src):
+        pltpu.make_async_copy(images.at[0], xbuf.at[img, src], recv_sem.at[img, src]).wait()
+
+    def first_norm(img, base, count):
+        for at in range(0, count * run, chunk):
+            span = pl.ds(pl.multiple_of(base * run + at, chunk), chunk)
+            put(h1, layer_norm(x_rows(img, at, base), ln1s[...], ln1b[...]), 8, rows=span)
+
+    def first_image(step, carry):
+        base = 2 * lax.rem(me // 2 + step, group // 2)
+        landed(0, base)
+        landed(0, base + 1)
+        first_norm(0, base, 2)
+        return carry
+
+    lax.fori_loop(0, group // 2, first_image, 0)
+
     def one_image(img, carry):
+        @pl.when(img + 1 < own)
+        def _():
+            send_image(img + 1, 0)
+
         first = img == 0
         last = img == own - 1
 
-        for src in range(group):
-            pltpu.make_async_copy(images.at[0], xbuf.at[img, src], recv_sem.at[img, src]).wait()
-
-        @pl.when(img + 1 < own)
-        def _():
-            send_image(img + 1, 0)
-
-        for at in range(0, rows, chunk):
-            put(hbuf, layer_norm(x_rows(img, at), ln1s[...], ln1b[...]), 8, rows=slice(at, at + chunk))
-
         @pl.when(first)
         def _():
             arrived(0)
 
         for c in range(3):
             weight = blocks(wqkv, 2, rows=slice(c * width, (c + 1) * width))
-            put(qkv, dot_t(blocks(hbuf, 8), weight) + bias[c:c + 1, :], 8, first=c * 8)
+            put(qkv, dot_t(blocks(h1, 8), weight) + bias[c:c + 1, :], 8, first=c * 8)
 
         lane = lax.broadcasted_iota(jnp.int32, (1, 128), 1)
         low = (lane < 64).astype(F32)
@@ -165,11 +176,11 @@
             ctx[hp] = (total / denom).astype(BF16)
 
         def head_pair(step, carry):
-            one_pair(2 * step)
-            one_pair(2 * step + 1)
+            for i in range(4):
+                one_pair(4 * step + i)
             return carry
 
-        lax.fori_loop(0, 4, head_pair, 0)
+        lax.fori_loop(0, 2, head_pair, 0)
 
         @pl.when(first)
         def _():
@@ -193,7 +204,15 @@
             arrived(3)
             arrived(4)
 
+        @pl.when(img + 1 < own)
+        def _():
+            for src in range(group):
+                landed(img + 1, src)
+
+        following = jnp.minimum(img + 1, own - 1)
+
         def hidden_chunk(step, carry):
+            first_norm(following, step * (group // 2), group // 2)
             spans = [pl.ds(pl.multiple_of((2 * step + i) * width, width), width) for i in range(2)]
             for i in range(2):
                 up = dot(blocks(hbuf, 8), blocks(wup, 2, first=(2 * step + i) * 2)) + bup[:, spans[i]]
@@ -248,7 +267,8 @@
     for c in range(4):
         up = dot(normed_out, blocks(wup, 2, first=c * 2)) + pbup[:, c * 1024:(c + 1) * 1024]
         total = total + dot(gelu(up).astype(BF16), blocks(wdown, 2, rows=slice(c * 1024, (c + 1) * 1024)))
-    emb[...] = total[:8]
+    for c in range(8):
+        emb[:, c, :] = total[:own, c * 128:(c + 1) * 128]
 
     def drain(img, carry):
         for step in range(1, group):
@@ -271,7 +291,8 @@
     for step in range(1, group):
         share(step).wait_send()
     for src in range(group):
-        out_ref[src * own:(src + 1) * own, :] = gath[src][:own]
+        for c in range(8):
+            out_ref[src * own:(src + 1) * own, c * 128:(c + 1) * 128] = gath[src, :, c, :]
 
 
 def solution(mesh):
@@ -300,6 +321,7 @@
                 pltpu.VMEM((2, 4 * width, 512), BF16),
                 pltpu.VMEM((2, 2 * width, 512), BF16),
                 pltpu.VMEM((8, rows, 128), BF16),
+                pltpu.VMEM((8, rows, 128), BF16),
                 pltpu.VMEM((24, rows, 128), BF16),
                 pltpu.VMEM((8, rows, 128), BF16),
                 pltpu.VMEM((16, rows, 128), BF16),
@@ -307,8 +329,8 @@
                 pltpu.VMEM((8, 128, 128), BF16),
                 pltpu.VMEM((8, width), F32),
                 pltpu.VMEM((16, width), F32),
-                pltpu.VMEM((8, width), F32),
-                pltpu.VMEM((group, 8, width), F32),
+                pltpu.VMEM((own, 8, 128), F32),
+                pltpu.VMEM((group, own, 8, 128), F32),
                 pltpu.SemaphoreType.DMA((own, group)),
                 pltpu.SemaphoreType.DMA((own, group)),
                 pltpu.SemaphoreType.DMA((9,)),

time: 159 us -> 155 us (0.975)
  Pallas kernels: 158 us -> 153 us
    pallas_call x1, Pallas kernels: 158 us -> 153 us  [device_step(): pl.pallas_call(functools.partial(kernel, group, own, run), out_shape=jax....]
where the time goes in v4:
time: 155 us
  Pallas kernels  153 us (99%)
  local copies, waits for them, and re-layouts  1.57 us (1%)
    pallas_call x1, Pallas kernels, device_step(): pl.pallas_call(functools.partial(kernel, group, own, run), out_shape=jax....  153 us

profile of v4, /device:TPU:0, one launch (start us, length us, event | category | flops | bytes accessed | tf_op | source)
XLA Modules:
  0.0 154.7 jit_solution(8718289137292127957)
XLA Ops:
  0.0 153.1 %shard_map.262 = f32[32,1024]{1,0:T(8,128)} custom-call(bf16[32,72,1024]{2,1,0:T(8,128)(2,1)} %images.1, f32[1,1024]{1,0:T(1,128)} %bitcast.34, f32[1,1024]{1,0:T(1,128)} %bitcast.35, f32[3,16,64]{2,1,0:T(8,128)} %bqkv_in.1, f32[1,1024]{1,0:T(1,128)} %bitcast.36, f32[1,1024]{1,0:T(1,128)} %bitcast.37, f32[1,1024]{1,0:T(1,128)} %bitcast.38, ...), custom_call_target="tpu_custom_call" | custom-call | tf_op jit(solution)/shard_map/pallas_call | solution.py:311
  153.1 1.6 %copy.30 = f32[32,1024]{1,0:T(8,128)} copy(f32[32,1024]{1,0:T(8,128)} %shard_map.262) | data formatting | bytes 262144

commit v5 on v4

--- a/solution.py
+++ b/solution.py
@@ -211,44 +211,41 @@
 
         following = jnp.minimum(img + 1, own - 1)
 
-        def hidden_chunk(step, carry):
-            first_norm(following, step * (group // 2), group // 2)
-            spans = [pl.ds(pl.multiple_of((2 * step + i) * width, width), width) for i in range(2)]
-            for i in range(2):
-                up = dot(blocks(hbuf, 8), blocks(wup, 2, first=(2 * step + i) * 2)) + bup[:, spans[i]]
-                put(mbuf, gelu(up), 8, first=8 * i)
-            acc[...] += dot(blocks(mbuf, 8), blocks(wdown, 2, rows=spans[0])) + dot(blocks(mbuf, 8, first=8), blocks(wdown, 2, rows=spans[1]))
-
-            @pl.when(last)
-            def _():
-                for i in range(4):
-                    part = step * 4 + i
-                    up_cols = pl.ds(pl.multiple_of(part * 512, 512), 512)
-                    pltpu.make_async_copy(pwup_hbm.at[:, up_cols], wup.at[part], w_sem.at[7]).start()
-                for i in range(2):
-                    down_rows = pl.ds(pl.multiple_of(step * 2 * width, width), 2 * width)
-                    pltpu.make_async_copy(pwdown_hbm.at[down_rows, i * 512:(i + 1) * 512], wdown.at[i, down_rows], w_sem.at[8]).start()
-
-            return carry
-
-        lax.fori_loop(0, 2, hidden_chunk, 0)
-
-        for at in range(0, rows, chunk):
-            block = slice(at, at + chunk)
-            y = acc[block, :].astype(BF16).astype(F32)
-            put(hbuf, layer_norm(y, lnfs[...], lnfb[...]), 8, rows=block)
+        for c in range(4):
+            up = dot(blocks(hbuf, 8), blocks(wup, 2, first=2 * c)) + bup[:, c * width:(c + 1) * width]
+            put(mbuf, gelu(up), 8, first=8 * c)
+            first_norm(following, 2 * c, 2)
+
+        @pl.when(last)
+        def _():
+            start(7)
+
+        for at in range(0, rows, rows // 2):
+            half = slice(at, at + rows // 2)
+            acc[half, :] = acc[half, :] + dot(blocks(mbuf, 32, rows=half), blocks(wdown, 2))
+            for sub in range(at, at + rows // 2, chunk):
+                block = slice(sub, sub + chunk)
+                y = acc[block, :].astype(BF16).astype(F32)
+                put(hbuf, layer_norm(y, lnfs[...], lnfb[...]), 8, rows=block)
+
+        @pl.when(last)
+        def _():
+            start(8)
 
         @pl.when(first)
         def _():
             arrived(5)
 
-        for c in range(2):
-            weight = blocks(pwkv, 2, rows=slice(c * width, (c + 1) * width))
-            put(qkv, dot_t(blocks(hbuf, 8), weight) + bias[3 + c:4 + c, :], 8, first=c * 8)
+        def pool_project(c):
+            rhs = blocks(pwkv, 2, rows=slice(c * width, (c + 1) * width))
+            put(qkv, dot_t(blocks(hbuf, 8), rhs) + bias[3 + c:4 + c, :], 8, first=c * 8)
+
+        pool_project(0)
         scores = dot_t(blocks(qkv, 8), blocks(ublk, 8))
         top = jnp.max(scores, axis=0, keepdims=True)
         weight = jnp.exp2((scores - top) * score_mul)
         wsum = jnp.sum(weight, axis=0, keepdims=True)
+        pool_project(1)
         value = lax.dot_general(weight.astype(BF16), blocks(qkv, 8, first=8), CONTRACT_FIRST, preferred_element_type=F32)[:16]
         diag = lax.broadcasted_iota(jnp.int32, (16, 128), 0) == lax.broadcasted_iota(jnp.int32, (16, 128), 1)
         wcol = jnp.sum(jnp.where(diag, jnp.broadcast_to(wsum, (16, 128)), 0.0), axis=1, keepdims=True)
@@ -324,7 +321,7 @@
                 pltpu.VMEM((8, rows, 128), BF16),
                 pltpu.VMEM((24, rows, 128), BF16),
                 pltpu.VMEM((8, rows, 128), BF16),
-                pltpu.VMEM((16, rows, 128), BF16),
+                pltpu.VMEM((32, rows, 128), BF16),
                 pltpu.VMEM((rows, width), F32),
                 pltpu.VMEM((8, 128, 128), BF16),
                 pltpu.VMEM((8, width), F32),

time: 155 us -> 149 us (0.961)
  Pallas kernels: 153 us -> 148 us
    pallas_call x1, Pallas kernels: 153 us -> 148 us  [device_step(): pl.pallas_call(functools.partial(kernel, group, own, run), out_shape=jax....]
where the time goes in v5:
time: 149 us
  Pallas kernels  148 us (99%)
  local copies, waits for them, and re-layouts  1.57 us (1%)
    pallas_call x1, Pallas kernels, device_step(): pl.pallas_call(functools.partial(kernel, group, own, run), out_shape=jax....  148 us

profile of v5, /device:TPU:0, one launch (start us, length us, event | category | flops | bytes accessed | tf_op | source)
XLA Modules:
  0.0 149.3 jit_solution(14056049008323670645)
XLA Ops:
  0.0 147.7 %shard_map.262 = f32[32,1024]{1,0:T(8,128)} custom-call(bf16[32,72,1024]{2,1,0:T(8,128)(2,1)} %images.1, f32[1,1024]{1,0:T(1,128)} %bitcast.34, f32[1,1024]{1,0:T(1,128)} %bitcast.35, f32[3,16,64]{2,1,0:T(8,128)} %bqkv_in.1, f32[1,1024]{1,0:T(1,128)} %bitcast.36, f32[1,1024]{1,0:T(1,128)} %bitcast.37, f32[1,1024]{1,0:T(1,128)} %bitcast.38, ...), custom_call_target="tpu_custom_call" | custom-call | tf_op jit(solution)/shard_map/pallas_call | solution.py:308
  147.7 1.6 %copy.30 = f32[32,1024]{1,0:T(8,128)} copy(f32[32,1024]{1,0:T(8,128)} %shard_map.262) | data formatting | bytes 262144

commit v6 on v5

--- a/solution.py
+++ b/solution.py
@@ -133,16 +133,17 @@
         base = 2 * lax.rem(me // 2 + step, group // 2)
         landed(0, base)
         landed(0, base + 1)
+        if own > 1:
+            @pl.when(step == group // 2 - 2)
+            def _():
+                send_image(1, 0)
+
         first_norm(0, base, 2)
         return carry
 
     lax.fori_loop(0, group // 2, first_image, 0)
 
     def one_image(img, carry):
-        @pl.when(img + 1 < own)
-        def _():
-            send_image(img + 1, 0)
-
         first = img == 0
         last = img == own - 1
 
@@ -185,6 +186,19 @@
         @pl.when(first)
         def _():
             arrived(2)
+            arrived(3)
+            arrived(4)
+
+        @pl.when(img + 1 < own)
+        def _():
+            for src in range(group):
+                landed(img + 1, src)
+
+        @pl.when(img + 2 < own)
+        def _():
+            send_image(img + 2, 0)
+
+        following = jnp.minimum(img + 1, own - 1)
 
         for at in range(0, rows, rows // 2):
             half = slice(at, at + rows // 2)
@@ -195,29 +209,17 @@
             acc[block, :] = r + bdown[...]
             put(hbuf, layer_norm(r, ln2s[...], ln2b[...]), 8, rows=block)
 
+        for c in range(4):
+            pieces = 2 if c == 0 else 1
+            for at in range(0, rows, rows // pieces):
+                part = slice(at, at + rows // pieces)
+                up = dot(blocks(hbuf, 8, rows=part), blocks(wup, 2, first=2 * c)) + bup[:, c * width:(c + 1) * width]
+                put(mbuf, gelu(up), 8, first=8 * c, rows=part)
+            first_norm(following, 2 * c, 2)
+
         @pl.when(last)
         def _():
             start(6)
-
-        @pl.when(first)
-        def _():
-            arrived(3)
-            arrived(4)
-
-        @pl.when(img + 1 < own)
-        def _():
-            for src in range(group):
-                landed(img + 1, src)
-
-        following = jnp.minimum(img + 1, own - 1)
-
-        for c in range(4):
-            up = dot(blocks(hbuf, 8), blocks(wup, 2, first=2 * c)) + bup[:, c * width:(c + 1) * width]
-            put(mbuf, gelu(up), 8, first=8 * c)
-            first_norm(following, 2 * c, 2)
-
-        @pl.when(last)
-        def _():
             start(7)
 
         for at in range(0, rows, rows // 2):

time: 149 us -> 148 us (level)
  Pallas kernels: 148 us -> 146 us
    pallas_call x1, Pallas kernels: 148 us -> 146 us  [device_step(): pl.pallas_call(functools.partial(kernel, group, own, run), out_shape=jax....]
where the time goes in v6:
time: 148 us
  Pallas kernels  146 us (99%)
  local copies, waits for them, and re-layouts  1.57 us (1%)
    pallas_call x1, Pallas kernels, device_step(): pl.pallas_call(functools.partial(kernel, group, own, run), out_shape=jax....  146 us

profile of v6, /device:TPU:0, one launch (start us, length us, event | category | flops | bytes accessed | tf_op | source)
XLA Modules:
  0.0 147.8 jit_solution(4853079532854699807)
XLA Ops:
  0.0 146.2 %shard_map.262 = f32[32,1024]{1,0:T(8,128)} custom-call(bf16[32,72,1024]{2,1,0:T(8,128)(2,1)} %images.1, f32[1,1024]{1,0:T(1,128)} %bitcast.34, f32[1,1024]{1,0:T(1,128)} %bitcast.35, f32[3,16,64]{2,1,0:T(8,128)} %bqkv_in.1, f32[1,1024]{1,0:T(1,128)} %bitcast.36, f32[1,1024]{1,0:T(1,128)} %bitcast.37, f32[1,1024]{1,0:T(1,128)} %bitcast.38, ...), custom_call_target="tpu_custom_call" | custom-call | tf_op jit(solution)/shard_map/pallas_call | solution.py:310
  146.2 1.6 %copy.30 = f32[32,1024]{1,0:T(8,128)} copy(f32[32,1024]{1,0:T(8,128)} %shard_map.262) | data formatting | bytes 262144
